TPU v7x, 32 devices: a whole 2x2x4 slice. The times are simulated.
32 devices in a mesh: dp: 8 (over z, x), tensor: 4 (over y, core).
Axes of the slice: x: 2, y: 2, z: 4, core: 2. Of those that a mesh axis runs over, the one named last changes fastest.
Arguments:
- tokens: bfloat16 [4096, 4608], P(('dp', 'tensor')), parts along dimension 0, may hold values from -6 to 6
- pre_gain: float32 [4608], replicated, may hold values from 0.1 to 1.9
- query_weight: bfloat16 [4608, 4096], P(None, 'tensor'), as said below
- key_weight: bfloat16 [4608, 2048], P(None, 'tensor'), as said below
- value_weight: bfloat16 [4608, 2048], P(None, 'tensor'), may hold values from -0.09375 to 0.09375
- out_weight: bfloat16 [4096, 4608], P('tensor'), may hold values from -0.09375 to 0.09375
- post_gain: float32 [4608], replicated, may hold values from 0.1 to 1.9
Outputs:
- layer_out: bfloat16 [4096, 4608], P(('dp', 'tensor')), parts along dimension 0
There are 8 independent parts, one for each index of `dp`. A program takes and returns all parts, laid end to end along the dimension named above; an argument that names none is the same for every part. Nothing has to cross between parts.
Inputs may be any that keep to these rules, and one draw needn't show every extreme that they name: `query_weight`: entries lie within 16 / sqrt(4608) of zero. `key_weight`: entries lie within 16 / sqrt(4608) of zero.
All inputs are finite; a program needn't handle non-finite values.
Results may differ from a plain program's by a relative error of at most 0.015.
Values may be sent and summed in bfloat16 or wider, within the bound.
A program may use at most 192 MiB of HBM per device.

v0:
```python
import functools

import jax
import jax.numpy as jnp
import numpy as np
from jax import lax
from jax.experimental import pallas as pl
from jax.experimental.pallas import tpu as pltpu
from jax.sharding import PartitionSpec as P

HEAD_DIM = 128
SEQ_LEN = 128


norm_epsilon = 1e-06
soft_cap = 50.0
query_scale = 1.0 / 12.0
rope_base = 10000.0


def rms_scale(vectors, scale_gain):
    mean_square = jnp.mean(vectors * vectors, axis=-1, keepdims=True)
    return vectors * lax.rsqrt(mean_square + norm_epsilon) * scale_gain


def rotate(vectors, positions):
    half_dim = vectors.shape[-1] // 2
    exponent = jnp.arange(half_dim, dtype=jnp.float32) / half_dim
    angles = positions.astype(jnp.float32)[:, None] * jnp.power(rope_base, -exponent)[None, :]
    cosine = jnp.cos(angles)[:, None, :]
    sine_part = jnp.sin(angles)[:, None, :]
    first_half = vectors[..., :half_dim]
    second_half = vectors[..., half_dim:]
    return jnp.concatenate(
        [
            first_half * cosine - second_half * sine_part,
            second_half * cosine + first_half * sine_part,
        ],
        axis=-1,
    )


def project_block(normed, query_weight, key_weight, value_weight):
    block_rows = normed.shape[0]
    positions = jnp.arange(block_rows, dtype=jnp.int32) % SEQ_LEN
    query = jnp.dot(normed, query_weight, preferred_element_type=jnp.float32)
    keys = jnp.dot(normed, key_weight, preferred_element_type=jnp.float32)
    values = jnp.dot(normed, value_weight, preferred_element_type=jnp.float32)
    query = rotate(query.reshape(block_rows, -1, HEAD_DIM), positions).reshape(block_rows, -1)
    keys = rotate(keys.reshape(block_rows, -1, HEAD_DIM), positions).reshape(block_rows, -1)
    return jnp.concatenate(
        [query.astype(jnp.bfloat16), keys.astype(jnp.bfloat16), values.astype(jnp.bfloat16)], axis=1
    )


def attend(query, keys, values, query_pos, key_pos):
    query_count = query.shape[0]
    key_count = keys.shape[0]
    key_heads = keys.shape[1] // HEAD_DIM
    groups = query.shape[1] // keys.shape[1]
    query_four = query.reshape(query_count, key_heads, groups, HEAD_DIM)
    key_three = keys.reshape(key_count, key_heads, HEAD_DIM)
    value_three = values.reshape(key_count, key_heads, HEAD_DIM)
    raw_scores = jnp.einsum(
        "qhgd,khd->hgqk", query_four, key_three, preferred_element_type=jnp.float32
    )
    capped = soft_cap * jnp.tanh(raw_scores * query_scale / soft_cap)
    allowed = jnp.logical_and(
        key_pos[None, :] <= query_pos[:, None],
        key_pos[None, :] // SEQ_LEN == query_pos[:, None] // SEQ_LEN,
    )
    weights = jnp.where(allowed[None, None], jnp.exp(capped), 0.0)
    probability = (weights / jnp.sum(weights, axis=-1, keepdims=True)).astype(jnp.bfloat16)
    mixed = jnp.einsum(
        "hgqk,khd->qhgd", probability, value_three, preferred_element_type=jnp.float32
    )
    return mixed.astype(jnp.bfloat16).reshape(query_count, -1)


def staged(tokens, pre_gain, query_weight, key_weight, value_weight, out_weight, post_gain):
    local_rows = tokens.shape[0]
    query_cols = query_weight.shape[1]
    key_cols = key_weight.shape[1]
    normed = rms_scale(tokens.astype(jnp.float32), pre_gain).astype(jnp.bfloat16)
    stacked = project_block(
        lax.all_gather(normed, "tensor", axis=0, tiled=True), query_weight, key_weight, value_weight
    )
    query = stacked[:, :query_cols]
    keys = stacked[:, query_cols : query_cols + key_cols]
    values = stacked[:, query_cols + key_cols :]
    token_count = stacked.shape[0]
    key_count = min(token_count, lax.axis_size("tensor") * local_rows + SEQ_LEN)
    key_first = jnp.clip(jnp.int32(0) // SEQ_LEN * SEQ_LEN, 0, token_count - key_count)
    query_pos = jnp.arange(lax.axis_size("tensor") * local_rows, dtype=jnp.int32)
    key_pos = key_first + jnp.arange(key_count, dtype=jnp.int32)
    block_out = attend(query, keys, values, query_pos, key_pos)
    mixed = lax.psum_scatter(
        jnp.dot(block_out, out_weight, preferred_element_type=jnp.float32).astype(jnp.bfloat16),
        "tensor",
        scatter_dimension=0,
        tiled=True,
    ).astype(jnp.float32)
    branch = rms_scale(mixed, post_gain)
    return (tokens.astype(jnp.float32) + branch).astype(jnp.bfloat16)


def rope_tables():
    half_dim = HEAD_DIM // 2
    angles = np.arange(SEQ_LEN)[:, None] * np.power(rope_base, -np.arange(half_dim) / half_dim)[None, :]
    cosine, sine = np.cos(angles), np.sin(angles)
    return np.stack(
        [np.concatenate([cosine, cosine], 1), np.concatenate([-sine, sine], 1)]
    ).astype(np.float32)


def divisor(count, wanted):
    return next(k for k in range(min(wanted, count), 0, -1) if count % k == 0)


def copy_to(src, dst, send_sem, recv_sem, index):
    return pltpu.make_async_remote_copy(
        src_ref=src,
        dst_ref=dst,
        send_sem=send_sem,
        recv_sem=recv_sem,
        device_id={"tensor": index},
        device_id_type=pl.DeviceIdType.MESH,
    )


def fused_kernel(
    cuts,
    row_cuts,
    tokens,
    pre_gain,
    query_weight,
    key_weight,
    value_weight,
    out_weight,
    post_gain,
    rope_table,
    out,
    xbuf,
    scaled,
    acc,
    square,
    weight,
    out_half,
    attended,
    part,
    local_in,
    remote_in,
    gain_pre,
    gain_post,
    rope,
    in_sem,
    w_sem,
    wo_sem,
    x_send,
    x_recv,
    link_send,
    link_recv,
    fwd_send,
    fwd_recv,
    att_send,
    att_recv,
    lp_send,
    lp_recv,
    rp_send,
    rp_recv,
):
    rows, width = tokens.shape
    q_cols = query_weight.shape[1]
    k_cols = key_weight.shape[1]
    all_cols = q_cols + 2 * k_cols
    half = width // 2
    chunk = half // cuts
    groups = q_cols // k_cols
    kv_heads = k_cols // HEAD_DIM
    step_rows = rows // row_cuts
    n_tile = all_cols // divisor(all_cols // 128, 4)
    o_tile = half // divisor(half // 128, 3)

    me = lax.axis_index("tensor")
    core = me % 2
    other = 1 - core
    side = me // 2
    mate = side * 2 + other
    far = (1 - side) * 2

    def cols(start, size):
        return pl.ds(pl.multiple_of(start, 128), size)

    def rws(start, size):
        return pl.ds(pl.multiple_of(start, 16), size)

    own = pltpu.make_async_copy(tokens, xbuf.at[rws(core * rows, rows)], in_sem.at[0])
    own.start()
    small = [
        pltpu.make_async_copy(pre_gain, gain_pre, in_sem.at[1]),
        pltpu.make_async_copy(post_gain, gain_post, in_sem.at[2]),
        pltpu.make_async_copy(rope_table, rope, in_sem.at[3]),
    ]
    for copy in small:
        copy.start()

    def weight_copies(k):
        at = pl.ds(pl.multiple_of(k * chunk, 128), chunk)
        return [
            pltpu.make_async_copy(query_weight.at[at], weight.at[at, 0:q_cols], w_sem.at[0, k]),
            pltpu.make_async_copy(key_weight.at[at], weight.at[at, q_cols : q_cols + k_cols], w_sem.at[1, k]),
            pltpu.make_async_copy(value_weight.at[at], weight.at[at, q_cols + k_cols : all_cols], w_sem.at[2, k]),
        ]

    barrier = pltpu.get_barrier_semaphore()
    for index in (mate, far, far + 1):
        pl.semaphore_signal(
            barrier, inc=1, device_id={"tensor": index}, device_id_type=pl.DeviceIdType.MESH
        )
    pl.semaphore_wait(barrier, 3)

    own.wait()

    def x_copy(owner, h, sem):
        ref = xbuf.at[rws(owner * rows, rows), cols(h * half, half)]
        return copy_to(ref, ref, x_send.at[sem], x_recv.at[sem], mate)

    x_copy(core, other, 0).start()
    x_copy(core, core, 1).start()

    def link_copy(s, j):
        at = cols(core * half + j * chunk, chunk)
        return copy_to(
            xbuf.at[pl.ds(s * rows, rows), at],
            xbuf.at[pl.ds((2 + s) * rows, rows), at],
            link_send.at[s, j],
            link_recv.at[s, j],
            far + core,
        )

    def send_link(s):
        for j in range(cuts):
            link_copy(s, j).start()

    @pl.when(core == 0)
    def _():
        send_link(0)

    for k in range(2 * cuts):
        for copy in weight_copies(k):
            copy.start()

    x_copy(other, core, 0).wait_recv()

    @pl.when(core == 1)
    def _():
        send_link(0)

    send_link(1)

    own_out = pltpu.make_async_copy(
        out_weight.at[:, cols(core * half, half)],
        out_half.at[rws(core * q_cols, q_cols)],
        in_sem.at[4],
    )
    own_out.start()
    push_out = copy_to(
        out_weight.at[:, cols(other * half, half)],
        out_half.at[rws(core * q_cols, q_cols)],
        wo_sem.at[0],
        wo_sem.at[1],
        mate,
    )
    push_out.start()
    x_copy(other, other, 1).wait_recv()
    for copy in small:
        copy.wait()

    def project(first_row, acc_row, count, k):
        ar = pl.ds(acc_row, count)
        at = cols(k * chunk, chunk)
        total = square[ar]
        for i in range(chunk // 128):
            x = xbuf[pl.ds(first_row, count), cols(k * chunk + i * 128, 128)].astype(jnp.float32)
            total = total + x * x
            gain = gain_pre[pl.ds(k * (chunk // 128) + i, 1)]
            scaled[0:count, i * 128 : (i + 1) * 128] = (x * gain).astype(jnp.bfloat16)
        square[ar] = total

        def tile(n, _):
            nat = cols(n * n_tile, n_tile)
            acc[ar, nat] += jnp.dot(
                scaled[0:count], weight[at, nat], preferred_element_type=jnp.float32
            )
            return 0

        lax.fori_loop(0, all_cols // n_tile, tile, 0)

    def clear(row, count):
        acc[pl.ds(row, count)] = jnp.zeros((count, all_cols), jnp.float32)
        square[pl.ds(row, count)] = jnp.zeros((count, 128), jnp.float32)

    def attend_slot(acc_row, slot):
        ar = pl.ds(acc_row, rows)
        scale = lax.rsqrt(
            jnp.sum(square[ar], axis=-1, keepdims=True) / width + norm_epsilon
        )
        cosine, sine = rope[0], rope[1]
        ok = lax.broadcasted_iota(jnp.int32, (rows, rows), 1) <= lax.broadcasted_iota(
            jnp.int32, (rows, rows), 0
        )
        ok = jnp.concatenate([ok] * groups, axis=0)

        def turned(at):
            v = acc[ar, at] * scale
            return (v * cosine + pltpu.roll(v, HEAD_DIM // 2, 1) * sine).astype(jnp.bfloat16)

        def head(g, _):
            query = jnp.concatenate(
                [turned(cols((g * groups + i) * HEAD_DIM, HEAD_DIM)) for i in range(groups)], axis=0
            )
            keys = turned(cols(q_cols + g * HEAD_DIM, HEAD_DIM))
            values = (acc[ar, cols(q_cols + k_cols + g * HEAD_DIM, HEAD_DIM)] * scale).astype(jnp.bfloat16)
            raw = lax.dot_general(
                query, keys, (((1,), (1,)), ((), ())), preferred_element_type=jnp.float32
            )
            capped = soft_cap * jnp.tanh(raw * (query_scale / soft_cap))
            mass = jnp.where(ok, jnp.exp(capped), 0.0)
            prob = (mass / jnp.sum(mass, axis=-1, keepdims=True)).astype(jnp.bfloat16)
            mixed = jnp.dot(prob, values, preferred_element_type=jnp.float32).astype(jnp.bfloat16)
            for i in range(groups):
                attended[
                    pl.ds(slot * rows, rows), cols(core * q_cols + (g * groups + i) * HEAD_DIM, HEAD_DIM)
                ] = mixed[i * rows : (i + 1) * rows]
            return 0

        lax.fori_loop(0, kv_heads, head, 0)

    def att_copy(slot, whose):
        ref = attended.at[pl.ds(slot * rows, rows), cols(whose * q_cols, q_cols)]
        return copy_to(ref, ref, att_send.at[slot], att_recv.at[slot], mate)

    def out_project(slot):
        def tile(n, _):
            at = cols(n * o_tile, o_tile)
            part[rws(slot * rows, rows), at] = jnp.dot(
                attended[rws(slot * rows, rows)], out_half[:, at], preferred_element_type=jnp.float32
            ).astype(jnp.bfloat16)
            return 0

        lax.fori_loop(0, half // o_tile, tile, 0)

    clear(0, 3 * rows)

    def local_step(k, _):
        for copy in weight_copies(k):
            copy.wait()
        project(0, 0, 2 * rows, k)
        return 0

    lax.fori_loop(0, 2 * cuts, local_step, 0)

    def arrived(s, j, h, send, recv, target):
        ref = xbuf.at[pl.ds((2 + s) * rows, rows), cols(h * half + j * chunk, chunk)]
        return copy_to(ref, ref, send.at[s, j], recv.at[s, j], target)

    def far_project(s):
        if s:
            clear(2 * rows, rows)

        def step(j, _):
            arrived(s, j, core, link_send, link_recv, far + core).wait_recv()
            arrived(s, j, core, fwd_send, fwd_recv, mate).start()
            project((2 + s) * rows, 2 * rows, rows, core * cuts + j)
            arrived(s, j, other, fwd_send, fwd_recv, mate).wait_recv()
            project((2 + s) * rows, 2 * rows, rows, other * cuts + j)
            return 0

        lax.fori_loop(0, cuts, step, 0)
        attend_slot(2 * rows, 2 + s)
        att_copy(2 + s, core).start()

    def part_copy(s, r):
        return copy_to(
            part.at[pl.ds((2 + s) * rows + r * step_rows, step_rows)],
            remote_in.at[pl.ds(r * step_rows, step_rows), cols(core * half, half)],
            rp_send.at[s, r],
            rp_recv.at[core, r],
            far + s,
        )

    def far_out(s):
        att_copy(2 + s, other).wait_recv()
        out_project(2 + s)
        for r in range(row_cuts):
            part_copy(s, r).start()

    far_project(0)
    own_out.wait()
    push_in = copy_to(
        out_half.at[rws(other * q_cols, q_cols)],
        out_half.at[rws(other * q_cols, q_cols)],
        wo_sem.at[0],
        wo_sem.at[1],
        mate,
    )
    push_in.wait_recv()
    far_out(0)

    far_project(1)
    far_out(1)

    for s in range(2):
        attend_slot(s * rows, s)
        att_copy(s, core).start()
    for s in range(2):
        att_copy(s, other).wait_recv()
    out_project(other)
    near_copy = copy_to(
        part.at[rws(other * rows, rows)], local_in, lp_send, lp_recv, mate
    )
    near_copy.start()
    out_project(core)

    near_copy.wait_recv()

    def finish(r, _):
        first = pl.multiple_of(r * step_rows, 16)
        at = pl.ds(first, step_rows)
        for h in range(2):
            ref = remote_in.at[at, h * half : (h + 1) * half]
            copy_to(ref, ref, rp_send.at[0, r], rp_recv.at[h, r], mate).wait_recv()
        own_at, other_at = cols(core * half, half), cols(other * half, half)
        near = part[rws(core * rows + r * step_rows, step_rows)].astype(jnp.float32)
        a = near + remote_in[at, own_at].astype(jnp.float32)
        b = local_in[at].astype(jnp.float32) + remote_in[at, other_at].astype(jnp.float32)
        total = jnp.sum(a * a, axis=-1, keepdims=True) + jnp.sum(b * b, axis=-1, keepdims=True)
        scale = lax.rsqrt(total / width + norm_epsilon)
        mine = rws(core * rows + r * step_rows, step_rows)
        for piece, h in ((a, core), (b, other)):
            piece = piece * scale
            for i in range(half // 128):
                where = cols(h * half + i * 128, 128)
                gain = gain_post[pl.ds(h * (half // 128) + i, 1)]
                out[at, where] = (
                    xbuf[mine, where].astype(jnp.float32) + piece[:, i * 128 : (i + 1) * 128] * gain
                ).astype(jnp.bfloat16)
        return 0

    lax.fori_loop(0, row_cuts, finish, 0)

    x_copy(core, other, 0).wait_send()
    x_copy(core, core, 1).wait_send()
    push_out.wait_send()
    near_copy.wait_send()
    for slot in range(4):
        att_copy(slot, core).wait_send()
    for s in range(2):
        for j in range(cuts):
            link_copy(s, j).wait_send()
            arrived(s, j, core, fwd_send, fwd_recv, mate).wait_send()
        for r in range(row_cuts):
            part_copy(s, r).wait_send()


def fused(tokens, pre_gain, query_weight, key_weight, value_weight, out_weight, post_gain):
    rows, width = tokens.shape
    q_cols = query_weight.shape[1]
    k_cols = key_weight.shape[1]
    all_cols = q_cols + 2 * k_cols
    half = width // 2
    cuts = divisor(half // 128, 3)
    row_cuts = divisor(rows // 16, 4)
    dma = pltpu.SemaphoreType.DMA
    bf16, f32 = jnp.bfloat16, jnp.float32
    return pl.pallas_call(
        functools.partial(fused_kernel, cuts, row_cuts),
        out_shape=pltpu.VMEM((rows, width), bf16),
        in_specs=[pl.BlockSpec(memory_space=pl.ANY)] * 8,
        out_specs=pl.BlockSpec(memory_space=pltpu.VMEM),
        scratch_shapes=[
            pltpu.VMEM((4 * rows, width), bf16),
            pltpu.VMEM((2 * rows, half // cuts), bf16),
            pltpu.VMEM((3 * rows, all_cols), f32),
            pltpu.VMEM((3 * rows, 128), f32),
            pltpu.VMEM((width, all_cols), bf16),
            pltpu.VMEM((2 * q_cols, half), bf16),
            pltpu.VMEM((4 * rows, 2 * q_cols), bf16),
            pltpu.VMEM((4 * rows, half), bf16),
            pltpu.VMEM((rows, half), bf16),
            pltpu.VMEM((rows, width), bf16),
            pltpu.VMEM((width // 128, 128), f32),
            pltpu.VMEM((width // 128, 128), f32),
            pltpu.VMEM((2, SEQ_LEN, HEAD_DIM), f32),
            dma((5,)),
            dma((3, 2 * cuts)),
            dma((2,)),
            dma((2,)),
            dma((2,)),
            dma((2, cuts)),
            dma((2, cuts)),
            dma((2, cuts)),
            dma((2, cuts)),
            dma((4,)),
            dma((4,)),
            dma,
            dma,
            dma((2, row_cuts)),
            dma((2, row_cuts)),
        ],
        compiler_params=pltpu.CompilerParams(
            collective_id=0, has_side_effects=True, vmem_limit_bytes=63_000_000
        ),
    )(
        tokens,
        pre_gain.reshape(width // 128, 128),
        query_weight,
        key_weight,
        value_weight,
        out_weight,
        post_gain.reshape(width // 128, 128),
        jnp.asarray(rope_tables()),
    )


def body(tokens, *rest):
    rows, width = tokens.shape
    four = lax.axis_size("tensor") == 4
    if four and rows == SEQ_LEN and width % 256 == 0:
        return fused(tokens, *rest)
    return staged(tokens, *rest)


def solution(mesh):
    return jax.shard_map(
        body,
        mesh=mesh,
        in_specs=(
            P(("dp", "tensor"), None),
            P(),
            P(None, "tensor"),
            P(None, "tensor"),
            P(None, "tensor"),
            P("tensor", None),
            P(),
        ),
        out_specs=P(("dp", "tensor"), None),
        check_vma=False,
    )
```

profile of v0, /device:TPU:1, one launch (start us, length us, event | category | flops | bytes accessed | tf_op | source)
XLA Modules:
  0.0 57.7 jit_solution(13346329654422440748)
XLA Ops:
  0.0 56.7 %shard_map.82 = bf16[128,4608]{1,0:T(8,128)(2,1)S(1)} custom-call(bf16[128,4608]{1,0:T(8,128)(2,1)} %tokens.1, f32[36,128]{1,0:T(8,128)} %bitcast.2, bf16[4608,1024]{1,0:T(8,128)(2,1)} %query_weight.1, bf16[4608,512]{1,0:T(8,128)(2,1)} %key_weight.1, bf16[4608,512]{1,0:T(8,128)(2,1)} %value_weight.1, bf16[1024,4608]{1,0:T(8,128)(2,1)} %out_weight.1, ...), custom_call_target="tpu_custom_call" | custom-call | tf_op jit(solution)/shard_map/pallas_call | solution.py:476
  56.7 1.0 %copy.10 = bf16[128,4608]{1,0:T(8,128)(2,1)} copy(bf16[128,4608]{1,0:T(8,128)(2,1)S(1)} %shard_map.82) | data formatting | bytes 2359296
where the time goes:
time: 57.9 us; the launch traced here: 57.7 us
  Pallas kernels  56.7 us (98%)
  local copies, waits for them, and re-layouts  1.02 us (2%)
    pallas_call x1, Pallas kernels, fused(): pl.pallas_call(functools.partial(fused_kernel, cuts, row_cuts), out_shape...  56.7 us

commit v1 on v0

--- a/solution.py
+++ b/solution.py
@@ -131,6 +131,8 @@
 def fused_kernel(
     cuts,
     row_cuts,
+    head_rows,
+    keep_rows,
     tokens,
     pre_gain,
     query_weight,
@@ -194,6 +196,12 @@
     def rws(start, size):
         return pl.ds(pl.multiple_of(start, 16), size)
 
+    def landed(ref, sem):
+        copy_to(ref, ref, sem, sem, mate).wait_recv()
+
+    def left(ref, sem):
+        copy_to(ref, ref, sem, sem, mate).wait_send()
+
     own = pltpu.make_async_copy(tokens, xbuf.at[rws(core * rows, rows)], in_sem.at[0])
     own.start()
     small = [
@@ -201,16 +209,20 @@
         pltpu.make_async_copy(post_gain, gain_post, in_sem.at[2]),
         pltpu.make_async_copy(rope_table, rope, in_sem.at[3]),
     ]
-    for copy in small:
-        copy.start()
-
-    def weight_copies(k):
-        at = pl.ds(pl.multiple_of(k * chunk, 128), chunk)
-        return [
-            pltpu.make_async_copy(query_weight.at[at], weight.at[at, 0:q_cols], w_sem.at[0, k]),
-            pltpu.make_async_copy(key_weight.at[at], weight.at[at, q_cols : q_cols + k_cols], w_sem.at[1, k]),
-            pltpu.make_async_copy(value_weight.at[at], weight.at[at, q_cols + k_cols : all_cols], w_sem.at[2, k]),
-        ]
+
+    def weight_rows(k):
+        return pl.ds(pl.multiple_of(k * chunk, 128), chunk)
+
+    def weight_start(k):
+        at = weight_rows(k)
+        sem = w_sem.at[k]
+        pltpu.make_async_copy(query_weight.at[at], weight.at[at, 0:q_cols], sem).start()
+        pltpu.make_async_copy(key_weight.at[at], weight.at[at, q_cols : q_cols + k_cols], sem).start()
+        pltpu.make_async_copy(value_weight.at[at], weight.at[at, q_cols + k_cols : all_cols], sem).start()
+
+    def weight_wait(k):
+        ref = weight.at[weight_rows(k)]
+        pltpu.make_async_copy(ref, ref, w_sem.at[k]).wait()
 
     barrier = pltpu.get_barrier_semaphore()
     for index in (mate, far, far + 1):
@@ -219,49 +231,86 @@
         )
     pl.semaphore_wait(barrier, 3)
 
-    own.wait()
-
     def x_copy(owner, h, sem):
         ref = xbuf.at[rws(owner * rows, rows), cols(h * half, half)]
-        return copy_to(ref, ref, x_send.at[sem], x_recv.at[sem], mate)
-
-    x_copy(core, other, 0).start()
-    x_copy(core, core, 1).start()
+        return copy_to(ref, ref, x_send.at[0], x_recv.at[sem], mate)
+
+    def far_chunk(s, j, h):
+        return xbuf.at[pl.ds((2 + s) * rows, rows), cols(h * half + j * chunk, chunk)]
+
+    def link_at(s, j, h, first, last, sem, source=None):
+        at = cols(h * half + j * chunk, chunk)
+        if source is None:
+            source = xbuf.at[pl.ds(s * rows + first, last - first), at]
+        return copy_to(
+            source,
+            xbuf.at[pl.ds((2 + s) * rows + first, last - first), at],
+            link_send.at[sem],
+            link_recv.at[s, j],
+            far + h,
+        )
 
     def link_copy(s, j):
-        at = cols(core * half + j * chunk, chunk)
-        return copy_to(
-            xbuf.at[pl.ds(s * rows, rows), at],
-            xbuf.at[pl.ds((2 + s) * rows, rows), at],
-            link_send.at[s, j],
-            link_recv.at[s, j],
-            far + core,
-        )
-
-    def send_link(s):
-        for j in range(cuts):
-            link_copy(s, j).start()
+        first = head_rows if j == 0 else 0
+        if s == 1 and j == cuts - 1:
+            return link_at(s, j, core, first, keep_rows, 2)
+        return link_at(s, j, core, first, rows, s)
+
+    def head_copy(s, source=None):
+        return link_at(s, 0, core, 0, head_rows, s, source)
+
+    def tail_copy(h):
+        return link_at(1, cuts - 1, h, keep_rows, rows, 3)
 
     @pl.when(core == 0)
     def _():
-        send_link(0)
-
-    for k in range(2 * cuts):
-        for copy in weight_copies(k):
-            copy.start()
-
-    x_copy(other, core, 0).wait_recv()
+        head_copy(0, tokens.at[0:head_rows, cols(core * half, chunk)]).start()
 
     @pl.when(core == 1)
     def _():
-        send_link(0)
-
-    send_link(1)
+        head_copy(1, tokens.at[0:head_rows, cols(core * half, chunk)]).start()
+
+    for copy in small:
+        copy.start()
+    own.wait()
+    x_copy(core, other, 0).start()
+
+    @pl.when(core == 0)
+    def _():
+        for j in range(cuts):
+            link_copy(0, j).start()
+
+    x_copy(core, core, 1).start()
+
+    def start_weights(k, _):
+        weight_start(k)
+        return 0
+
+    lax.fori_loop(0, 2 * cuts, start_weights, 0)
+
+    x_copy(other, core, 0).wait_recv()
+
+    @pl.when(core == 1)
+    def _():
+        head_copy(0).start()
+        for j in range(cuts):
+            link_copy(0, j).start()
+        for j in range(cuts - 1):
+            link_copy(1, j).start()
+        tail_copy(0).start()
+        link_copy(1, cuts - 1).start()
+        tail_copy(1).start()
+
+    @pl.when(core == 0)
+    def _():
+        head_copy(1).start()
+        for j in range(cuts):
+            link_copy(1, j).start()
 
     own_out = pltpu.make_async_copy(
         out_weight.at[:, cols(core * half, half)],
         out_half.at[rws(core * q_cols, q_cols)],
-        in_sem.at[4],
+        in_sem.at[0],
     )
     own_out.start()
     push_out = copy_to(
@@ -294,14 +343,14 @@
             )
             return 0
 
-        lax.fori_loop(0, all_cols // n_tile, tile, 0)
+        lax.fori_loop(0, all_cols // n_tile, tile, 0, unroll=True)
 
     def clear(row, count):
         acc[pl.ds(row, count)] = jnp.zeros((count, all_cols), jnp.float32)
         square[pl.ds(row, count)] = jnp.zeros((count, 128), jnp.float32)
 
     def attend_slot(acc_row, slot):
-        ar = pl.ds(acc_row, rows)
+        ar = rws(acc_row, rows)
         scale = lax.rsqrt(
             jnp.sum(square[ar], axis=-1, keepdims=True) / width + norm_epsilon
         )
@@ -330,7 +379,7 @@
             mixed = jnp.dot(prob, values, preferred_element_type=jnp.float32).astype(jnp.bfloat16)
             for i in range(groups):
                 attended[
-                    pl.ds(slot * rows, rows), cols(core * q_cols + (g * groups + i) * HEAD_DIM, HEAD_DIM)
+                    rws(slot * rows, rows), cols(core * q_cols + (g * groups + i) * HEAD_DIM, HEAD_DIM)
                 ] = mixed[i * rows : (i + 1) * rows]
             return 0
 
@@ -338,7 +387,7 @@
 
     def att_copy(slot, whose):
         ref = attended.at[pl.ds(slot * rows, rows), cols(whose * q_cols, q_cols)]
-        return copy_to(ref, ref, att_send.at[slot], att_recv.at[slot], mate)
+        return copy_to(ref, ref, att_send.at[0], att_recv.at[max(slot - 1, 0)], mate)
 
     def out_project(slot):
         def tile(n, _):
@@ -348,44 +397,35 @@
             ).astype(jnp.bfloat16)
             return 0
 
-        lax.fori_loop(0, half // o_tile, tile, 0)
+        lax.fori_loop(0, half // o_tile, tile, 0, unroll=True)
 
     clear(0, 3 * rows)
 
     def local_step(k, _):
-        for copy in weight_copies(k):
-            copy.wait()
+        weight_wait(k)
         project(0, 0, 2 * rows, k)
         return 0
 
     lax.fori_loop(0, 2 * cuts, local_step, 0)
 
-    def arrived(s, j, h, send, recv, target):
-        ref = xbuf.at[pl.ds((2 + s) * rows, rows), cols(h * half + j * chunk, chunk)]
-        return copy_to(ref, ref, send.at[s, j], recv.at[s, j], target)
-
-    def far_project(s):
-        if s:
-            clear(2 * rows, rows)
-
-        def step(j, _):
-            arrived(s, j, core, link_send, link_recv, far + core).wait_recv()
-            arrived(s, j, core, fwd_send, fwd_recv, mate).start()
-            project((2 + s) * rows, 2 * rows, rows, core * cuts + j)
-            arrived(s, j, other, fwd_send, fwd_recv, mate).wait_recv()
-            project((2 + s) * rows, 2 * rows, rows, other * cuts + j)
-            return 0
-
-        lax.fori_loop(0, cuts, step, 0)
-        attend_slot(2 * rows, 2 + s)
-        att_copy(2 + s, core).start()
+    def passed(s, j, h):
+        ref = far_chunk(s, j, h)
+        sem = cuts if s == 1 and j == 0 else j
+        return copy_to(ref, ref, fwd_send.at[0], fwd_recv.at[sem], mate)
+
+    def far_step(s, j):
+        landed(far_chunk(s, j, core), link_recv.at[s, j])
+        passed(s, j, core).start()
+        project((2 + s) * rows, 2 * rows, rows, core * cuts + j)
+        passed(s, j, other).wait_recv()
+        project((2 + s) * rows, 2 * rows, rows, other * cuts + j)
 
     def part_copy(s, r):
         return copy_to(
             part.at[pl.ds((2 + s) * rows + r * step_rows, step_rows)],
             remote_in.at[pl.ds(r * step_rows, step_rows), cols(core * half, half)],
-            rp_send.at[s, r],
-            rp_recv.at[core, r],
+            rp_send.at[0],
+            rp_recv.at[r],
             far + s,
         )
 
@@ -395,26 +435,24 @@
         for r in range(row_cuts):
             part_copy(s, r).start()
 
-    far_project(0)
+    for j in range(cuts):
+        far_step(0, j)
+    attend_slot(2 * rows, 2)
+    att_copy(2, core).start()
+    clear(2 * rows, rows)
     own_out.wait()
-    push_in = copy_to(
-        out_half.at[rws(other * q_cols, q_cols)],
-        out_half.at[rws(other * q_cols, q_cols)],
-        wo_sem.at[0],
-        wo_sem.at[1],
-        mate,
-    )
-    push_in.wait_recv()
+    landed(out_half.at[rws(other * q_cols, q_cols)], wo_sem.at[1])
     far_out(0)
-
-    far_project(1)
+    for j in range(cuts):
+        far_step(1, j)
+    attend_slot(2 * rows, 3)
+    att_copy(3, core).start()
     far_out(1)
-
-    for s in range(2):
-        attend_slot(s * rows, s)
-        att_copy(s, core).start()
-    for s in range(2):
-        att_copy(s, other).wait_recv()
+    attend_slot(0, 0)
+    att_copy(0, core).start()
+    attend_slot(rows, 1)
+    att_copy(1, core).start()
+    landed(attended.at[0 : 2 * rows, cols(other * q_cols, q_cols)], att_recv.at[0])
     out_project(other)
     near_copy = copy_to(
         part.at[rws(other * rows, rows)], local_in, lp_send, lp_recv, mate
@@ -422,14 +460,25 @@
     near_copy.start()
     out_project(core)
 
+    left(xbuf.at[rws(core * rows, rows)], x_send.at[0])
+    push_out.wait_send()
+    left(xbuf.at[0:rows, cols(core * half, half)], link_send.at[0])
+    left(xbuf.at[0:rows, cols(core * half, half - chunk)], link_send.at[1])
+    left(xbuf.at[0:keep_rows, cols(core * half, chunk)], link_send.at[2])
+
+    @pl.when(core == 1)
+    def _():
+        left(xbuf.at[0 : rows - keep_rows, 0 : 2 * chunk], link_send.at[3])
+
+    left(xbuf.at[2 * rows : 4 * rows, cols(core * half, half)], fwd_send.at[0])
+    left(attended.at[:, cols(core * q_cols, q_cols)], att_send.at[0])
+    near_copy.wait_send()
     near_copy.wait_recv()
 
     def finish(r, _):
         first = pl.multiple_of(r * step_rows, 16)
         at = pl.ds(first, step_rows)
-        for h in range(2):
-            ref = remote_in.at[at, h * half : (h + 1) * half]
-            copy_to(ref, ref, rp_send.at[0, r], rp_recv.at[h, r], mate).wait_recv()
+        landed(remote_in.at[at], rp_recv.at[r])
         own_at, other_at = cols(core * half, half), cols(other * half, half)
         near = part[rws(core * rows + r * step_rows, step_rows)].astype(jnp.float32)
         a = near + remote_in[at, own_at].astype(jnp.float32)
@@ -448,19 +497,7 @@
         return 0
 
     lax.fori_loop(0, row_cuts, finish, 0)
-
-    x_copy(core, other, 0).wait_send()
-    x_copy(core, core, 1).wait_send()
-    push_out.wait_send()
-    near_copy.wait_send()
-    for slot in range(4):
-        att_copy(slot, core).wait_send()
-    for s in range(2):
-        for j in range(cuts):
-            link_copy(s, j).wait_send()
-            arrived(s, j, core, fwd_send, fwd_recv, mate).wait_send()
-        for r in range(row_cuts):
-            part_copy(s, r).wait_send()
+    left(part.at[2 * rows : 4 * rows], rp_send.at[0])
 
 
 def fused(tokens, pre_gain, query_weight, key_weight, value_weight, out_weight, post_gain):
@@ -470,11 +507,13 @@
     all_cols = q_cols + 2 * k_cols
     half = width // 2
     cuts = divisor(half // 128, 3)
-    row_cuts = divisor(rows // 16, 4)
+    row_cuts = divisor(rows // 16, 8)
+    head_rows = rows // 2
+    keep_rows = rows // 2
     dma = pltpu.SemaphoreType.DMA
     bf16, f32 = jnp.bfloat16, jnp.float32
     return pl.pallas_call(
-        functools.partial(fused_kernel, cuts, row_cuts),
+        functools.partial(fused_kernel, cuts, row_cuts, head_rows, keep_rows),
         out_shape=pltpu.VMEM((rows, width), bf16),
         in_specs=[pl.BlockSpec(memory_space=pl.ANY)] * 8,
         out_specs=pl.BlockSpec(memory_space=pltpu.VMEM),
@@ -492,21 +531,21 @@
             pltpu.VMEM((width // 128, 128), f32),
             pltpu.VMEM((width // 128, 128), f32),
             pltpu.VMEM((2, SEQ_LEN, HEAD_DIM), f32),
-            dma((5,)),
-            dma((3, 2 * cuts)),
+            dma((4,)),
+            dma((2 * cuts,)),
             dma((2,)),
+            dma((1,)),
             dma((2,)),
-            dma((2,)),
+            dma((4,)),
             dma((2, cuts)),
-            dma((2, cuts)),
-            dma((2, cuts)),
-            dma((2, cuts)),
-            dma((4,)),
-            dma((4,)),
+            dma((1,)),
+            dma((cuts + 1,)),
+            dma((1,)),
+            dma((3,)),
             dma,
             dma,
-            dma((2, row_cuts)),
-            dma((2, row_cuts)),
+            dma((1,)),
+            dma((row_cuts,)),
         ],
         compiler_params=pltpu.CompilerParams(
             collective_id=0, has_side_effects=True, vmem_limit_bytes=63_000_000
@@ -526,7 +565,7 @@
 def body(tokens, *rest):
     rows, width = tokens.shape
     four = lax.axis_size("tensor") == 4
-    if four and rows == SEQ_LEN and width % 256 == 0:
+    if four and rows == SEQ_LEN and width % 768 == 0:
         return fused(tokens, *rest)
     return staged(tokens, *rest)
 

time: 57.9 us -> 56.2 us (0.971)
  Pallas kernels: 56.7 us -> 55 us
    pallas_call x1, Pallas kernels: 56.7 us -> 55 us  [fused(): pl.pallas_call(functools.partial(fused_kernel, cuts, row_cuts, head_rows,...]
where the time goes in v1:
time: 56.2 us; the launch traced here: 56.1 us
  Pallas kernels  55 us (98%)
  local copies, waits for them, and re-layouts  1.02 us (2%)
    pallas_call x1, Pallas kernels, fused(): pl.pallas_call(functools.partial(fused_kernel, cuts, row_cuts, head_rows,...  55 us

profile of v1, /device:TPU:1, one launch (start us, length us, event | category | flops | bytes accessed | tf_op | source)
XLA Modules:
  0.0 56.1 jit_solution(2412574447354608868)
XLA Ops:
  0.0 55.0 %shard_map.82 = bf16[128,4608]{1,0:T(8,128)(2,1)S(1)} custom-call(bf16[128,4608]{1,0:T(8,128)(2,1)} %tokens.1, f32[36,128]{1,0:T(8,128)} %bitcast.2, bf16[4608,1024]{1,0:T(8,128)(2,1)} %query_weight.1, bf16[4608,512]{1,0:T(8,128)(2,1)} %key_weight.1, bf16[4608,512]{1,0:T(8,128)(2,1)} %value_weight.1, bf16[1024,4608]{1,0:T(8,128)(2,1)} %out_weight.1, ...), custom_call_target="tpu_custom_call" | custom-call | tf_op jit(solution)/shard_map/pallas_call | solution.py:515
  55.0 1.0 %copy.10 = bf16[128,4608]{1,0:T(8,128)(2,1)} copy(bf16[128,4608]{1,0:T(8,128)(2,1)S(1)} %shard_map.82) | data formatting | bytes 2359296

commit v2 on v1

--- a/solution.py
+++ b/solution.py
@@ -128,9 +128,15 @@
     )
 
 
+def sent_rows(rows, width, q_cols, all_cols, chunk):
+    half = width // 2
+    total = rows * width + q_cols * half + 4 * rows * q_cols + 7 * rows * half - rows * chunk
+    return total // all_cols if total % (16 * all_cols) == 0 else 0
+
+
 def fused_kernel(
     cuts,
-    row_cuts,
+    pieces,
     head_rows,
     keep_rows,
     tokens,
@@ -157,18 +163,13 @@
     rope,
     in_sem,
     w_sem,
-    wo_sem,
-    x_send,
+    sent,
+    tail_sent,
     x_recv,
-    link_send,
+    out_recv,
     link_recv,
-    fwd_send,
     fwd_recv,
-    att_send,
     att_recv,
-    lp_send,
-    lp_recv,
-    rp_send,
     rp_recv,
 ):
     rows, width = tokens.shape
@@ -179,7 +180,7 @@
     chunk = half // cuts
     groups = q_cols // k_cols
     kv_heads = k_cols // HEAD_DIM
-    step_rows = rows // row_cuts
+    step_rows = 16
     n_tile = all_cols // divisor(all_cols // 128, 4)
     o_tile = half // divisor(half // 128, 3)
 
@@ -206,8 +207,8 @@
     own.start()
     small = [
         pltpu.make_async_copy(pre_gain, gain_pre, in_sem.at[1]),
-        pltpu.make_async_copy(post_gain, gain_post, in_sem.at[2]),
-        pltpu.make_async_copy(rope_table, rope, in_sem.at[3]),
+        pltpu.make_async_copy(post_gain, gain_post, in_sem.at[1]),
+        pltpu.make_async_copy(rope_table, rope, in_sem.at[1]),
     ]
 
     def weight_rows(k):
@@ -215,52 +216,55 @@
 
     def weight_start(k):
         at = weight_rows(k)
-        sem = w_sem.at[k]
+        sem = w_sem.at[k // 2]
         pltpu.make_async_copy(query_weight.at[at], weight.at[at, 0:q_cols], sem).start()
         pltpu.make_async_copy(key_weight.at[at], weight.at[at, q_cols : q_cols + k_cols], sem).start()
         pltpu.make_async_copy(value_weight.at[at], weight.at[at, q_cols + k_cols : all_cols], sem).start()
 
     def weight_wait(k):
-        ref = weight.at[weight_rows(k)]
+        ref = weight.at[pl.ds(pl.multiple_of(2 * k * chunk, 128), 2 * chunk)]
         pltpu.make_async_copy(ref, ref, w_sem.at[k]).wait()
 
     barrier = pltpu.get_barrier_semaphore()
-    for index in (mate, far, far + 1):
+    for index in (mate, far + core):
         pl.semaphore_signal(
             barrier, inc=1, device_id={"tensor": index}, device_id_type=pl.DeviceIdType.MESH
         )
-    pl.semaphore_wait(barrier, 3)
+    pl.semaphore_wait(barrier, 2)
 
     def x_copy(owner, h, sem):
         ref = xbuf.at[rws(owner * rows, rows), cols(h * half, half)]
-        return copy_to(ref, ref, x_send.at[0], x_recv.at[sem], mate)
+        return copy_to(ref, ref, sent, x_recv.at[sem], mate)
 
     def far_chunk(s, j, h):
         return xbuf.at[pl.ds((2 + s) * rows, rows), cols(h * half + j * chunk, chunk)]
 
-    def link_at(s, j, h, first, last, sem, source=None):
+    def link_sem(s, j):
+        return 2 * s + (j == cuts - 1)
+
+    def link_at(s, j, h, first, last, sem=None, source=None):
         at = cols(h * half + j * chunk, chunk)
         if source is None:
             source = xbuf.at[pl.ds(s * rows + first, last - first), at]
         return copy_to(
             source,
             xbuf.at[pl.ds((2 + s) * rows + first, last - first), at],
-            link_send.at[sem],
-            link_recv.at[s, j],
+            sent if sem is None else sem,
+            link_recv.at[link_sem(s, j)],
             far + h,
         )
 
     def link_copy(s, j):
         first = head_rows if j == 0 else 0
         if s == 1 and j == cuts - 1:
-            return link_at(s, j, core, first, keep_rows, 2)
-        return link_at(s, j, core, first, rows, s)
+            return link_at(s, j, core, first, keep_rows, tail_sent)
+        return link_at(s, j, core, first, rows)
 
     def head_copy(s, source=None):
-        return link_at(s, 0, core, 0, head_rows, s, source)
+        return link_at(s, 0, core, 0, head_rows, source=source)
 
     def tail_copy(h):
-        return link_at(1, cuts - 1, h, keep_rows, rows, 3)
+        return link_at(1, cuts - 1, h, keep_rows, rows, tail_sent)
 
     @pl.when(core == 0)
     def _():
@@ -297,7 +301,6 @@
             link_copy(0, j).start()
         for j in range(cuts - 1):
             link_copy(1, j).start()
-        tail_copy(0).start()
         link_copy(1, cuts - 1).start()
         tail_copy(1).start()
 
@@ -316,14 +319,14 @@
     push_out = copy_to(
         out_weight.at[:, cols(other * half, half)],
         out_half.at[rws(core * q_cols, q_cols)],
-        wo_sem.at[0],
-        wo_sem.at[1],
+        sent,
+        out_recv,
         mate,
     )
     push_out.start()
     x_copy(other, other, 1).wait_recv()
-    for copy in small:
-        copy.wait()
+    small_ref = acc.at[0 : 2 * gain_pre.shape[0] + 2 * SEQ_LEN, 0:128]
+    pltpu.make_async_copy(small_ref, small_ref, in_sem.at[1]).wait()
 
     def project(first_row, acc_row, count, k):
         ar = pl.ds(acc_row, count)
@@ -387,7 +390,7 @@
 
     def att_copy(slot, whose):
         ref = attended.at[pl.ds(slot * rows, rows), cols(whose * q_cols, q_cols)]
-        return copy_to(ref, ref, att_send.at[0], att_recv.at[max(slot - 1, 0)], mate)
+        return copy_to(ref, ref, sent, att_recv.at[int(slot == 3)], mate)
 
     def out_project(slot):
         def tile(n, _):
@@ -403,48 +406,65 @@
 
     def local_step(k, _):
         weight_wait(k)
-        project(0, 0, 2 * rows, k)
+        for i in range(2):
+            project(0, 0, 2 * rows, 2 * k + i)
         return 0
 
-    lax.fori_loop(0, 2 * cuts, local_step, 0)
-
-    def passed(s, j, h):
-        ref = far_chunk(s, j, h)
-        sem = cuts if s == 1 and j == 0 else j
-        return copy_to(ref, ref, fwd_send.at[0], fwd_recv.at[sem], mate)
-
-    def far_step(s, j):
-        landed(far_chunk(s, j, core), link_recv.at[s, j])
-        passed(s, j, core).start()
-        project((2 + s) * rows, 2 * rows, rows, core * cuts + j)
-        passed(s, j, other).wait_recv()
-        project((2 + s) * rows, 2 * rows, rows, other * cuts + j)
-
-    def part_copy(s, r):
+    lax.fori_loop(0, cuts, local_step, 0)
+
+    def far_cols(s, last, h):
+        first = cuts - 1 if last else 0
+        count = 1 if last else cuts - 1
+        return xbuf.at[
+            pl.ds((2 + s) * rows, rows), cols(h * half + first * chunk, count * chunk)
+        ]
+
+    def passed(s, last, h):
+        ref = far_cols(s, last, h)
+        return copy_to(ref, ref, sent, fwd_recv.at[2 * s + last], mate)
+
+    def far_step(s, last):
+        landed(far_cols(s, last, core), link_recv.at[2 * s + last])
+        if s == 0 and not last:
+
+            @pl.when(core == 1)
+            def _():
+                tail_copy(0).start()
+
+        passed(s, last, core).start()
+        which = range(cuts - 1, cuts) if last else range(cuts - 1)
+        for j in which:
+            project((2 + s) * rows, 2 * rows, rows, core * cuts + j)
+        passed(s, last, other).wait_recv()
+        for j in which:
+            project((2 + s) * rows, 2 * rows, rows, other * cuts + j)
+
+    def part_copy(s, p):
+        at = pl.ds(sum(pieces[:p]), pieces[p])
         return copy_to(
-            part.at[pl.ds((2 + s) * rows + r * step_rows, step_rows)],
-            remote_in.at[pl.ds(r * step_rows, step_rows), cols(core * half, half)],
-            rp_send.at[0],
-            rp_recv.at[r],
+            part.at[pl.ds((2 + s) * rows + sum(pieces[:p]), pieces[p])],
+            remote_in.at[at, cols(core * half, half)],
+            sent,
+            rp_recv.at[p],
             far + s,
         )
 
     def far_out(s):
         att_copy(2 + s, other).wait_recv()
         out_project(2 + s)
-        for r in range(row_cuts):
-            part_copy(s, r).start()
-
-    for j in range(cuts):
-        far_step(0, j)
+        for p in range(len(pieces)):
+            part_copy(s, p).start()
+
+    for last in range(2):
+        far_step(0, last)
     attend_slot(2 * rows, 2)
     att_copy(2, core).start()
     clear(2 * rows, rows)
     own_out.wait()
-    landed(out_half.at[rws(other * q_cols, q_cols)], wo_sem.at[1])
+    landed(out_half.at[rws(other * q_cols, q_cols)], out_recv)
     far_out(0)
-    for j in range(cuts):
-        far_step(1, j)
+    for last in range(2):
+        far_step(1, last)
     attend_slot(2 * rows, 3)
     att_copy(3, core).start()
     far_out(1)
@@ -455,30 +475,16 @@
     landed(attended.at[0 : 2 * rows, cols(other * q_cols, q_cols)], att_recv.at[0])
     out_project(other)
     near_copy = copy_to(
-        part.at[rws(other * rows, rows)], local_in, lp_send, lp_recv, mate
+        part.at[rws(other * rows, rows)], local_in, sent, out_recv, mate
     )
     near_copy.start()
     out_project(core)
 
-    left(xbuf.at[rws(core * rows, rows)], x_send.at[0])
-    push_out.wait_send()
-    left(xbuf.at[0:rows, cols(core * half, half)], link_send.at[0])
-    left(xbuf.at[0:rows, cols(core * half, half - chunk)], link_send.at[1])
-    left(xbuf.at[0:keep_rows, cols(core * half, chunk)], link_send.at[2])
-
-    @pl.when(core == 1)
-    def _():
-        left(xbuf.at[0 : rows - keep_rows, 0 : 2 * chunk], link_send.at[3])
-
-    left(xbuf.at[2 * rows : 4 * rows, cols(core * half, half)], fwd_send.at[0])
-    left(attended.at[:, cols(core * q_cols, q_cols)], att_send.at[0])
-    near_copy.wait_send()
     near_copy.wait_recv()
 
     def finish(r, _):
         first = pl.multiple_of(r * step_rows, 16)
         at = pl.ds(first, step_rows)
-        landed(remote_in.at[at], rp_recv.at[r])
         own_at, other_at = cols(core * half, half), cols(other * half, half)
         near = part[rws(core * rows + r * step_rows, step_rows)].astype(jnp.float32)
         a = near + remote_in[at, own_at].astype(jnp.float32)
@@ -496,8 +502,20 @@
                 ).astype(jnp.bfloat16)
         return 0
 
-    lax.fori_loop(0, row_cuts, finish, 0)
-    left(part.at[2 * rows : 4 * rows], rp_send.at[0])
+    for p, count in enumerate(pieces):
+        first = sum(pieces[:p])
+        landed(remote_in.at[pl.ds(first, count)], rp_recv.at[p])
+        lax.fori_loop(first // step_rows, (first + count) // step_rows, finish, 0)
+
+    left(weight.at[0 : sent_rows(rows, width, q_cols, all_cols, chunk)], sent)
+
+    @pl.when(core == 0)
+    def _():
+        left(xbuf.at[0:keep_rows, 0:chunk], tail_sent)
+
+    @pl.when(core == 1)
+    def _():
+        left(xbuf.at[0 : 2 * rows - keep_rows, 0:chunk], tail_sent)
 
 
 def fused(tokens, pre_gain, query_weight, key_weight, value_weight, out_weight, post_gain):
@@ -506,14 +524,14 @@
     k_cols = key_weight.shape[1]
     all_cols = q_cols + 2 * k_cols
     half = width // 2
-    cuts = divisor(half // 128, 3)
-    row_cuts = divisor(rows // 16, 8)
+    cuts = 3
+    pieces = (3 * rows // 8, 3 * rows // 8, rows // 8, rows // 8)
     head_rows = rows // 2
     keep_rows = rows // 2
     dma = pltpu.SemaphoreType.DMA
     bf16, f32 = jnp.bfloat16, jnp.float32
     return pl.pallas_call(
-        functools.partial(fused_kernel, cuts, row_cuts, head_rows, keep_rows),
+        functools.partial(fused_kernel, cuts, pieces, head_rows, keep_rows),
         out_shape=pltpu.VMEM((rows, width), bf16),
         in_specs=[pl.BlockSpec(memory_space=pl.ANY)] * 8,
         out_specs=pl.BlockSpec(memory_space=pltpu.VMEM),
@@ -531,21 +549,16 @@
             pltpu.VMEM((width // 128, 128), f32),
             pltpu.VMEM((width // 128, 128), f32),
             pltpu.VMEM((2, SEQ_LEN, HEAD_DIM), f32),
-            dma((4,)),
-            dma((2 * cuts,)),
             dma((2,)),
-            dma((1,)),
-            dma((2,)),
-            dma((4,)),
-            dma((2, cuts)),
-            dma((1,)),
-            dma((cuts + 1,)),
-            dma((1,)),
-            dma((3,)),
+            dma((cuts,)),
             dma,
             dma,
-            dma((1,)),
-            dma((row_cuts,)),
+            dma((2,)),
+            dma,
+            dma((4,)),
+            dma((4,)),
+            dma((2,)),
+            dma((len(pieces),)),
         ],
         compiler_params=pltpu.CompilerParams(
             collective_id=0, has_side_effects=True, vmem_limit_bytes=63_000_000
@@ -564,9 +577,11 @@
 
 def body(tokens, *rest):
     rows, width = tokens.shape
+    q_cols, all_cols = rest[1].shape[1], sum(w.shape[1] for w in rest[1:4])
     four = lax.axis_size("tensor") == 4
     if four and rows == SEQ_LEN and width % 768 == 0:
-        return fused(tokens, *rest)
+        if sent_rows(rows, width, q_cols, all_cols, width // 6):
+            return fused(tokens, *rest)
     return staged(tokens, *rest)
 
 

time: 56.2 us -> 56 us (level)
  no operation moved by 1% of the time
where the time goes in v2:
time: 56 us; the launch traced here: 55.9 us
  Pallas kernels  54.9 us (98%)
  local copies, waits for them, and re-layouts  1.02 us (2%)
    pallas_call x1, Pallas kernels, fused(): pl.pallas_call(functools.partial(fused_kernel, cuts, pieces, head_rows, k...  54.9 us

profile of v2, /device:TPU:1, one launch (start us, length us, event | category | flops | bytes accessed | tf_op | source)
XLA Modules:
  0.0 55.9 jit_solution(9871333212604530460)
XLA Ops:
  0.0 54.9 %shard_map.82 = bf16[128,4608]{1,0:T(8,128)(2,1)S(1)} custom-call(bf16[128,4608]{1,0:T(8,128)(2,1)} %tokens.1, f32[36,128]{1,0:T(8,128)} %bitcast.2, bf16[4608,1024]{1,0:T(8,128)(2,1)} %query_weight.1, bf16[4608,512]{1,0:T(8,128)(2,1)} %key_weight.1, bf16[4608,512]{1,0:T(8,128)(2,1)} %value_weight.1, bf16[1024,4608]{1,0:T(8,128)(2,1)} %out_weight.1, ...), custom_call_target="tpu_custom_call" | custom-call | tf_op jit(solution)/shard_map/pallas_call | solution.py:533
  54.9 1.0 %copy.10 = bf16[128,4608]{1,0:T(8,128)(2,1)} copy(bf16[128,4608]{1,0:T(8,128)(2,1)S(1)} %shard_map.82) | data formatting | bytes 2359296
